TPU v7x, 32 devices: a whole 2x2x4 slice. The times are simulated.
32 devices in a mesh: pipe: 4 (over z), expert: 4 (over y, x), tensor: 2 (over core).
Axes of the slice: x: 2, y: 2, z: 4, core: 2. Of those that a mesh axis runs over, the one named last changes fastest.
Arguments:
- inputs_prev: bfloat16 [4, 512, 3584], P('pipe', 'expert', 'tensor'), may hold values from -6 to 6
- cotangent_next: bfloat16 [4, 512, 3584], P('pipe', 'expert', 'tensor'), may hold values from -6 to 6
- saved_input: bfloat16 [4, 512, 3584], P('pipe', 'expert', 'tensor'), may hold values from -6 to 6
- expert_ids: int32 [2, 4, 512, 8], P(None, 'pipe', 'expert'), may hold values from 0 to 255, as said below
- keep_mask: int32 [2, 4, 512, 8], P(None, 'pipe', 'expert'), may hold values from 0 to 1, as said below
- slot_pos: int32 [2, 4, 512, 8], P(None, 'pipe', 'expert'), may hold values from 0 to 3, as said below
- weight_q: int32 [2, 4, 512, 8], P(None, 'pipe', 'expert'), may hold values from 1 to 4095
- gate_routed: bfloat16 [4, 4, 3584, 512], P('pipe', 'expert', None, 'tensor'), may hold values from -0.09375 to 0.09375
- up_routed: bfloat16 [4, 4, 3584, 512], P('pipe', 'expert', None, 'tensor'), may hold values from -0.09375 to 0.09375
- down_routed: bfloat16 [4, 4, 512, 3584], P('pipe', 'expert', 'tensor'), may hold values from -0.1875 to 0.1875
- gate_shared: bfloat16 [4, 3584, 1024], P('pipe', None, 'tensor'), may hold values from -0.09375 to 0.09375
- up_shared: bfloat16 [4, 3584, 1024], P('pipe', None, 'tensor'), may hold values from -0.09375 to 0.09375
- down_shared: bfloat16 [4, 1024, 3584], P('pipe', 'tensor'), may hold values from -0.1875 to 0.1875
Outputs:
- out_act: bfloat16 [4, 512, 3584], P('pipe', 'expert', 'tensor')
- in_grad: bfloat16 [4, 512, 3584], P('pipe', 'expert', 'tensor')
Inputs may be any that keep to these rules, and one draw needn't show every extreme that they name: `expert_ids`: each row names 8 different experts; in every section and micro-batch one expert below 2 is named by every row. `keep_mask`: 1 only where the expert named is below 2; in one block of 128 rows no expert has more than 4 kept choices, and in every section and micro-batch one expert has exactly 4 in every block. `slot_pos`: kept choices of one block naming the same expert hold different slots; 0 where keep_mask is 0.
All inputs are finite; a program needn't handle non-finite values.
Results may differ from a plain program's by a relative error of at most 0.005.
Values may be sent and summed in bfloat16 or wider, within the bound.
A program may use at most 64 MiB of HBM per device.

v0:
```python
import jax
import jax.numpy as jnp
from jax import lax
from jax.sharding import PartitionSpec as P


def passed_along(block, axis, distance):
    devices = range(lax.axis_size(axis))
    route = [((i - distance) % len(devices), i) for i in devices]
    return lax.ppermute(block, axis, route)


def swish(values):
    return values * jax.nn.sigmoid(values)


def swish_slope(values):
    logistic = jax.nn.sigmoid(values)
    return logistic * (1.0 + values * (1.0 - logistic))


def contract_last(left, right):
    return lax.dot_general(
        left, right, (((1,), (1,)), ((), ())), preferred_element_type=jnp.float32
    )


def slot_plan(choice_ids, kept_flags, slot_index, weight_levels, total_slots, capacity):
    target = jnp.where(kept_flags > 0, choice_ids * capacity + slot_index, -1)
    slots = jnp.arange(total_slots, dtype=jnp.int32)
    match = target[None] == slots[:, None, None]
    chosen = jnp.sum(match.astype(jnp.int32), axis=2)
    level = jnp.sum(jnp.where(match, weight_levels[None], 0), axis=2)
    return (chosen.astype(jnp.bfloat16), level)


def section_link(values, offset):
    return passed_along(values, "pipe", offset)


def select_rows(chosen, values):
    return jnp.dot(chosen, values, preferred_element_type=jnp.float32)


def split_level(level):
    high = (level // 64).astype(jnp.float32) / 64.0
    low = (level % 64).astype(jnp.float32) / 4096.0
    return (high.astype(jnp.bfloat16), low.astype(jnp.bfloat16))


def combine(factors, rows):
    return lax.dot_general(
        factors, rows, (((0,), (0,)), ((), ())), preferred_element_type=jnp.float32
    )


def other_sums(total, n_tensor):
    width = total.shape[1] // n_tensor
    me = lax.axis_index("tensor")
    mine = lax.dynamic_slice_in_dim(total, me * width, width, axis=1)
    for step in range(1, n_tensor):
        to = (me + step) % n_tensor
        piece = lax.dynamic_slice_in_dim(total, to * width, width, axis=1)
        mine = mine + passed_along(piece, "tensor", step)
    return mine


def expert_local(rows_in, rows_saved, rows_cot, gate_w, up_w, down_w):
    gate_pre = jnp.dot(rows_in, gate_w, preferred_element_type=jnp.float32)
    up_pre = jnp.dot(rows_in, up_w, preferred_element_type=jnp.float32)
    hidden = (swish(gate_pre) * up_pre).astype(jnp.bfloat16)
    result = jnp.dot(hidden, down_w, preferred_element_type=jnp.float32).astype(jnp.bfloat16)
    gate_back = jnp.dot(rows_saved, gate_w, preferred_element_type=jnp.float32)
    up_back = jnp.dot(rows_saved, up_w, preferred_element_type=jnp.float32)
    grad_hidden = contract_last(rows_cot, down_w)
    grad_gate = (grad_hidden * up_back * swish_slope(gate_back)).astype(jnp.bfloat16)
    grad_up = (grad_hidden * swish(gate_back)).astype(jnp.bfloat16)
    grad_rows = (contract_last(grad_gate, gate_w) + contract_last(grad_up, up_w)).astype(
        jnp.bfloat16
    )
    return (result, grad_rows)


def shared_pass(full_in, full_saved, full_cot, gate_w, up_w, down_w):
    gate_pre = jnp.dot(full_in, gate_w, preferred_element_type=jnp.float32)
    up_pre = jnp.dot(full_in, up_w, preferred_element_type=jnp.float32)
    hidden = (swish(gate_pre) * up_pre).astype(jnp.bfloat16)
    shared_out = jnp.dot(hidden, down_w, preferred_element_type=jnp.float32)
    gate_back = jnp.dot(full_saved, gate_w, preferred_element_type=jnp.float32)
    up_back = jnp.dot(full_saved, up_w, preferred_element_type=jnp.float32)
    grad_hidden = contract_last(full_cot, down_w)
    grad_gate = (grad_hidden * up_back * swish_slope(gate_back)).astype(jnp.bfloat16)
    grad_up = (grad_hidden * swish(gate_back)).astype(jnp.bfloat16)
    shared_grad = contract_last(grad_gate, gate_w) + contract_last(grad_up, up_w)
    return (shared_out, shared_grad)


def local(
    inputs_prev,
    cotangent_next,
    saved_input,
    expert_ids,
    keep_mask,
    slot_pos,
    weight_q,
    gate_routed,
    up_routed,
    down_routed,
    gate_shared,
    up_shared,
    down_shared,
):
    capacity = inputs_prev.shape[1] // 32
    n_expert = lax.axis_size("expert")
    n_tensor = lax.axis_size("tensor")
    experts_here = n_expert // 2
    slots = experts_here * capacity
    forward_in = section_link(inputs_prev[0], 1)
    backward_in = section_link(cotangent_next[0], -1)
    chosen_f, level_f = slot_plan(
        expert_ids[0, 0], keep_mask[0, 0], slot_pos[0, 0], weight_q[0, 0], slots, capacity
    )
    chosen_b, level_b = slot_plan(
        expert_ids[1, 0], keep_mask[1, 0], slot_pos[1, 0], weight_q[1, 0], slots, capacity
    )
    gate_w = gate_routed[0, 0]
    up_w = up_routed[0, 0]
    down_w = down_routed[0, 0]
    full_saved = lax.all_gather(saved_input[0], "tensor", axis=1, tiled=True)
    full_in = lax.all_gather(forward_in, "tensor", axis=1, tiled=True)
    full_cot = lax.all_gather(backward_in, "tensor", axis=1, tiled=True)
    feature_count = full_in.shape[1]
    weight_b = jnp.sum(level_b, axis=1).astype(jnp.float32) / 4096.0
    parcel = jnp.stack(
        (
            select_rows(chosen_f, full_in).astype(jnp.bfloat16),
            select_rows(chosen_b, full_saved).astype(jnp.bfloat16),
            (weight_b[:, None] * select_rows(chosen_b, full_cot)).astype(jnp.bfloat16),
        )
    ).reshape(3, experts_here, 1, capacity, feature_count)
    parcel = jnp.broadcast_to(parcel, (3, experts_here, 2, capacity, feature_count))
    parcel = parcel.reshape(3, n_expert, capacity, feature_count)
    pieces = lax.all_to_all(parcel, "expert", split_axis=1, concat_axis=1, tiled=True)
    rows = pieces.reshape(3, n_expert * capacity, feature_count)
    result, grad_rows = expert_local(rows[0], rows[1], rows[2], gate_w, up_w, down_w)
    returned = lax.all_to_all(
        jnp.stack((result, grad_rows)).reshape(2, n_expert, capacity, feature_count),
        "expert",
        split_axis=1,
        concat_axis=1,
        tiled=True,
    )
    back = returned.reshape(2, n_expert * capacity, feature_count)

    def doubled(factors):
        spread = factors.reshape(experts_here, 1, capacity, -1)
        spread = jnp.broadcast_to(spread, (experts_here, 2) + spread.shape[2:])
        return spread.reshape(n_expert * capacity, -1)

    high_f, low_f = split_level(level_f)
    factors_f = jnp.concatenate((doubled(high_f), doubled(low_f)), axis=0)
    routed_out = combine(factors_f, jnp.concatenate((back[0], back[0]), axis=0))
    routed_grad = combine(doubled(chosen_b), back[1])
    shared_out, shared_grad = shared_pass(
        full_in, full_saved, full_cot, gate_shared[0], up_shared[0], down_shared[0]
    )
    summed_out = other_sums(routed_out + shared_out, n_tensor)
    summed_grad = other_sums(routed_grad + shared_grad, n_tensor)
    return (summed_out.astype(jnp.bfloat16)[None], summed_grad.astype(jnp.bfloat16)[None])


def solution(mesh):
    return jax.shard_map(
        local,
        mesh=mesh,
        in_specs=(
            P("pipe", "expert", "tensor"),
            P("pipe", "expert", "tensor"),
            P("pipe", "expert", "tensor"),
            P(None, "pipe", "expert", None),
            P(None, "pipe", "expert", None),
            P(None, "pipe", "expert", None),
            P(None, "pipe", "expert", None),
            P("pipe", "expert", None, "tensor"),
            P("pipe", "expert", None, "tensor"),
            P("pipe", "expert", "tensor", None),
            P("pipe", None, "tensor"),
            P("pipe", None, "tensor"),
            P("pipe", "tensor", None),
        ),
        out_specs=(P("pipe", "expert", "tensor"), P("pipe", "expert", "tensor")),
        check_vma=False,
    )
```

profile of v0, /device:TPU:0, one launch (start us, length us, event | category | flops | bytes accessed | tf_op | source)
XLA Modules:
  0.0 99.7 jit_solution(14145739943017148776)
XLA Ops:
  0.6 0.0 copy-start
  0.6 5.1 %collective-permute-start.1 = (bf16[128,1792]{1,0:T(8,128)(2,1)}, bf16[128,1792]{1,0:T(8,128)(2,1)}, u32[]{:S(2)}, u32[]{:S(2)}) collective-permute-start(bf16[128,1792]{1,0:T(8,128)(2,1)} %bitcast.127), channel_id=1, source_target_pairs={{8,0},{16,8},{24,16},{0,24},{9,1},{17,9},{25,17},{1,25},{10,2},{18... | collective-permute-start | bytes 1376264 | tf_op jit(solution)/shard_map/ppermute | solution.py:10
  5.8 0.8 slice_bitcast_fusion.1
  6.6 0.2 select_reduce_fusion
  6.8 2.7 %all-gather = bf16[1,128,3584]{2,1,0:T(8,128)(2,1)S(1)} all-gather(bf16[1,128,1792]{2,1,0:T(8,128)(2,1)} %param.15), channel_id=2, replica_groups=mesh['pipe'=4,'expert'=4,'tensor'=2] {'tensor'}, dimensions={2}, use_global_device_ids=true | all-gather | bytes 1376256 | tf_op jit(solution)/shard_map/all_gather | solution.py:129
  9.6 0.2 convolution_convert_fusion.1
  9.8 2.7 %fusion.13 = f32[128,512]{1,0:T(8,128)S(1)} fusion(bf16[1,3584,512]{2,1,0:T(8,128)(2,1)} %param.23, bf16[1,128,3584]{2,1,0:T(8,128)(2,1)S(1)} %all-gather), kind=kOutput, calls=%fused_computation.20 | convolution fusion | flops 469762048 | bytes 4849664 | tf_op jit(solution)/shard_map/dot_general | solution.py:89
  12.5 4.5 %collective-permute-done.1 = bf16[128,1792]{1,0:T(8,128)(2,1)} collective-permute-done((bf16[128,1792]{1,0:T(8,128)(2,1)}, bf16[128,1792]{1,0:T(8,128)(2,1)}, u32[]{:S(2)}, u32[]{:S(2)}) %collective-permute-start.1) | collective-permute-done | bytes 458784 | tf_op jit(solution)/shard_map/ppermute | solution.py:10
  17.0 2.7 %all_gather.11 = bf16[128,3584]{1,0:T(8,128)(2,1)S(1)} all-gather(bf16[128,1792]{1,0:T(8,128)(2,1)} %collective-permute-done.1), channel_id=1, replica_groups=mesh['pipe'=4,'expert'=4,'tensor'=2] {'tensor'}, dimensions={1}, use_global_device_ids=true | all-gather | bytes 1376256 | tf_op jit(solution)/shard_map/all_gather | solution.py:131
  19.7 0.9 fusion.2
  20.6 1.5 %stack.23 = bf16[1,2,1,4,3584]{4,3,1,2,0:T(4,128)(2,1)} reshape(bf16[8,3584]{1,0:T(8,128)(2,1)} %fusion.2) | data formatting | bytes 114688 | tf_op jit(solution)/shard_map/stack | solution.py:134
  22.1 4.4 %collective-permute-done = bf16[128,1792]{1,0:T(8,128)(2,1)S(1)} collective-permute-done((bf16[128,1792]{1,0:T(8,128)(2,1)}, bf16[128,1792]{1,0:T(8,128)(2,1)S(1)}, u32[]{:S(2)}, u32[]{:S(2)}) %collective-permute-start) | collective-permute-done | bytes 458784 | tf_op jit(solution)/shard_map/ppermute | solution.py:10
  26.5 2.5 %all_gather.9 = bf16[128,3584]{1,0:T(8,128)(2,1)S(1)} all-gather(bf16[128,1792]{1,0:T(8,128)(2,1)S(1)} %collective-permute-done), channel_id=1, replica_groups=mesh['pipe'=4,'expert'=4,'tensor'=2] {'tensor'}, dimensions={1}, use_global_device_ids=true | all-gather | bytes 1376256 | tf_op jit(solution)/shard_map/all_gather | solution.py:130
  29.0 0.2 convolution_convert_fusion.2
  29.2 1.0 maximum_bitcast_fusion
  30.2 0.1 copy.26
  30.2 0.8 broadcast_in_dim.69
  31.1 4.1 %all-to-all-start = ((bf16[3,4,4,3584]{3,2,0,1:T(4,128)(2,1)}), bf16[3,4,4,3584]{3,2,0,1:T(4,128)(2,1)}, u32[]{:S(2)}, u32[]{:S(2)}) async-start(bf16[3,4,4,3584]{3,2,0,1:T(4,128)(2,1)} %bitcast.11), calls=%async_computation | async-start | bytes 688128 | tf_op jit(solution)/shard_map/all_to_all | solution.py:143
  35.2 3.6 %fusion.3 = f32[128,512]{1,0:T(8,128)S(1)} fusion(bf16[128,3584]{1,0:T(8,128)(2,1)} %copy-done.3, bf16[1,512,3584]{2,1,0:T(8,128)(2,1)} %param.25), kind=kOutput, calls=%fused_computation.10 | convolution fusion | flops 469762048 | bytes 4849664 | tf_op jit(solution)/shard_map/dot_general | solution.py:23
  38.8 6.6 %fusion.11 = f32[128,3584]{1,0:T(8,128)} fusion(bf16[1,3584,512]{2,1,0:T(8,128)(2,1)} %param.23, f32[128,512]{1,0:T(8,128)S(1)} %fusion.3, bf16[1,3584,512]{2,1,0:T(8,128)(2,1)} %param.24, bf16[1,128,3584]{2,1,0:T(8,128)(2,1)} %copy-done.2, f32[128,512]{1,0:T(8,128)S(1)} %fusion.13), kind=kOutput, calls=%fused_computation.18 | convolution fusion | flops 940179456 | bytes 10616832 | tf_op jit(solution)/shard_map/dot_general | solution.py:23
  45.4 1.8 %fusion.112 = (bf16[1,4,4,3584]{3,2,0,1:T(4,128)(2,1)}, bf16[1,4,4,3584]{3,2,0,1:T(4,128)(2,1)S(1)}, bf16[1,4,4,3584]{3,2,0,1:T(4,128)(2,1)S(1)}) fusion(bf16[3,4,4,3584]{3,2,0,1:T(4,128)(2,1)} %all-to-all-done), kind=kLoop, calls=%fused_computation.123 | loop fusion | bytes 688128 | tf_op jit(solution)/shard_map/slice | solution.py:145
  47.1 0.7 squeeze.56
  47.9 2.2 %fusion.17 = f32[16,256]{1,0:T(8,128)S(1)} fusion(bf16[16,3584]{1,0:T(8,128)(2,1)} %squeeze.56, bf16[1,1,256,3584]{3,2,1,0:T(8,128)(2,1)} %param.22), kind=kOutput, calls=%fused_computation.24 | convolution fusion | flops 29360128 | bytes 1966080 | tf_op jit(solution)/shard_map/dot_general | solution.py:23
  50.1 0.4 fusion.27
  50.5 3.5 %fusion.25 = f32[16,3584]{1,0:T(8,128)} fusion(bf16[1,1,3584,256]{3,2,1,0:T(8,128)(2,1)} %param.20, f32[16,256]{1,0:T(8,128)S(1)} %fusion.17, bf16[16,3584]{1,0:T(8,128)(2,1)S(1)} %squeeze.57, bf16[1,1,3584,256]{3,2,1,0:T(8,128)(2,1)S(1)} %copy-done, f32[16,256]{1,0:T(8,128)S(1)} %fusion.27), kind=kOutput, calls=%fused_computation.32 | convolution fusion | flops 58761216 | bytes 4046848 | tf_op jit(solution)/shard_map/dot_general | solution.py:23
  54.0 1.5 %fusion.1 = bf16[16,3584]{1,0:T(8,128)(2,1)S(1)} fusion(f32[16,3584]{1,0:T(8,128)} %fusion.25, bf16[1,1,3584,256]{3,2,1,0:T(8,128)(2,1)S(1)} %copy-done, f32[16,256]{1,0:T(8,128)S(1)} %fusion.17, f32[16,256]{1,0:T(8,128)S(1)} %fusion.27), kind=kOutput, calls=%fused_computation.4 | convolution fusion | flops 29499392 | bytes 2211840 | tf_op jit(solution)/shard_map/dot_general | solution.py:23
  55.5 0.9 squeeze.52
  56.5 1.8 %fusion.29 = f32[16,256]{1,0:T(8,128)S(1)} fusion(bf16[16,3584]{1,0:T(8,128)(2,1)S(1)} %squeeze.52, bf16[1,1,3584,256]{3,2,1,0:T(8,128)(2,1)} %param.20), kind=kOutput, calls=%fused_computation.36 | convolution fusion | flops 29360128 | bytes 1966080 | tf_op jit(solution)/shard_map/dot_general | solution.py:69
  58.3 3.3 %convolution_convert_fusion = bf16[16,3584]{1,0:T(8,128)(2,1)} fusion(bf16[1,1,256,3584]{3,2,1,0:T(8,128)(2,1)} %param.22, bf16[16,3584]{1,0:T(8,128)(2,1)S(1)} %squeeze.52, bf16[1,1,3584,256]{3,2,1,0:T(8,128)(2,1)S(1)} %copy-done, f32[16,256]{1,0:T(8,128)S(1)} %fusion.29), kind=kOutput, calls=%fused_computation.5 | convolution fusion | flops 58802176 | bytes 3915776 | tf_op jit(solution)/shard_map/dot_general | solution.py:72
  61.6 0.9 stack.25
  62.5 0.8 pad_maximum_fusion
  63.4 4.1 %all-to-all-start.1 = ((bf16[2,4,4,3584]{3,2,0,1:T(4,128)(2,1)}), bf16[2,4,4,3584]{3,2,0,1:T(4,128)(2,1)}, u32[]{:S(2)}, u32[]{:S(2)}) async-start(bf16[2,4,4,3584]{3,2,0,1:T(4,128)(2,1)} %pad_maximum_fusion), calls=%async_computation.1 | async-start | bytes 458752 | tf_op jit(solution)/shard_map/all_to_all | solution.py:146
  67.5 2.7 %fusion.9 = f32[128,512]{1,0:T(8,128)S(1)} fusion(bf16[128,3584]{1,0:T(8,128)(2,1)S(1)} %all_gather.9, bf16[1,3584,512]{2,1,0:T(8,128)(2,1)} %param.24), kind=kOutput, calls=%fused_computation.16 | convolution fusion | flops 469762048 | bytes 4849664 | tf_op jit(solution)/shard_map/dot_general | solution.py:86
  70.2 3.0 %all-to-all-done.1 = bf16[2,4,4,3584]{3,2,0,1:T(4,128)(2,1)} async-done(((bf16[2,4,4,3584]{3,2,0,1:T(4,128)(2,1)}), bf16[2,4,4,3584]{3,2,0,1:T(4,128)(2,1)}, u32[]{:S(2)}, u32[]{:S(2)}) %all-to-all-start.1) | async-done | bytes 229408 | tf_op jit(solution)/shard_map/all_to_all | solution.py:146
  73.2 1.7 %fusion.113 = (bf16[1,4,4,3584]{3,2,0,1:T(4,128)(2,1)}, bf16[1,4,4,3584]{3,2,0,1:T(4,128)(2,1)}) fusion(bf16[2,4,4,3584]{3,2,0,1:T(4,128)(2,1)} %all-to-all-done.1), kind=kLoop, calls=%fused_computation.124 | loop fusion | bytes 458752 | tf_op jit(solution)/shard_map/slice | solution.py:163
  74.9 1.6 %squeeze.58 = bf16[16,3584]{1,0:T(8,128)(2,1)} reshape(bf16[1,4,4,3584]{3,2,0,1:T(4,128)(2,1)} %get-tuple-element.10) | data formatting | bytes 229376 | tf_op jit(solution)/shard_map/squeeze | solution.py:162
  76.5 2.6 %fusion.71 = f32[128,3584]{1,0:T(8,128)} fusion(bf16[16,3584]{1,0:T(8,128)(2,1)} %squeeze.58, bf16[16,128]{1,0:T(8,128)(2,1)S(1)} %bitcast.123, bf16[16,128]{1,0:T(8,128)(2,1)S(1)} %bitcast.124), kind=kOutput, calls=%fused_computation.61 | convolution fusion | flops 29835264 | bytes 1957888 | tf_op jit(solution)/shard_map/dot_general | solution.py:52
  79.1 6.2 %convolution_add_fusion.1 = f32[128,3584]{1,0:T(8,128)} fusion(f32[128,3584]{1,0:T(8,128)} %fusion.71, bf16[1,512,3584]{2,1,0:T(8,128)(2,1)} %param.25, f32[128,512]{1,0:T(8,128)S(1)} %fusion.9, bf16[128,3584]{1,0:T(8,128)(2,1)S(1)} %all_gather.9, bf16[1,3584,512]{2,1,0:T(8,128)(2,1)} %param.23), kind=kOutput, calls=%fused_computation.2 | convolution fusion | flops 940376064 | bytes 12189696 | tf_op jit(solution)/shard_map/dot_general | solution.py:88
  85.3 2.2 %constant_dynamic-slice_fusion = f32[128,1792]{1,0:T(8,128)} fusion(f32[128,3584]{1,0:T(8,128)} %convolution_add_fusion.1, s32[]{:T(128)S(6)} %select_n.74), kind=kLoop, calls=%fused_computation.113 | loop fusion | bytes 1835012 | tf_op jit(solution)/shard_map/dynamic_slice | solution.py:63
  87.6 0.4 fusion.114
  88.0 1.1 %copy-done.6 = f32[128,3584]{1,0:T(8,128)S(1)} copy-done((f32[128,3584]{1,0:T(8,128)S(1)}, f32[128,3584]{1,0:T(8,128)}, u32[]{:S(2)}) %copy-start.6) | copy-done | bytes 1835032
  89.1 3.4 %fusion = f32[128,3584]{1,0:T(8,128)S(1)} fusion(f32[128,3584]{1,0:T(8,128)S(1)} %fusion.114, f32[128,3584]{1,0:T(8,128)S(1)} %copy-done.6, bf16[1,3584,512]{2,1,0:T(8,128)(2,1)} %param.24, f32[128,512]{1,0:T(8,128)S(1)} %fusion.3, f32[128,512]{1,0:T(8,128)S(1)} %fusion.13), kind=kOutput, calls=%fused_computation.1 | convolution fusion | flops 471072768 | bytes 9699328 | tf_op jit(solution)/shard_map/dot_general | solution.py:23
  92.5 1.3 %copy-done.4 = f32[128,3584]{1,0:T(8,128)} copy-done((f32[128,3584]{1,0:T(8,128)}, f32[128,3584]{1,0:T(8,128)S(1)}, u32[]{:S(2)}) %copy-start.4) | copy-done | bytes 1835032
  93.7 1.0 %constant_dynamic-slice_fusion.1 = f32[128,1792]{1,0:T(8,128)} fusion(f32[128,3584]{1,0:T(8,128)S(1)} %fusion, s32[]{:T(128)S(6)} %select_n.74), kind=kLoop, calls=%fused_computation.114 | loop fusion | bytes 1835012 | tf_op jit(solution)/shard_map/dynamic_slice | solution.py:63
  94.7 0.5 collective-permute-start.3
  95.2 2.2 %fusion.65 = bf16[1,128,1792]{2,1,0:T(8,128)(2,1)} fusion(f32[128,1792]{1,0:T(8,128)S(1)} %collective-permute-done.2, f32[128,3584]{1,0:T(8,128)} %convolution_add_fusion.1, s32[]{:T(128)S(6)} %select_n.72), kind=kLoop, calls=%fused_computation.51 | loop fusion | flops 458752 | bytes 2293764 | tf_op jit(solution)/shard_map/broadcast_in_dim | solution.py:169
  97.4 0.3 collective-permute-done.3
  97.7 2.0 %fusion.66 = bf16[1,128,1792]{2,1,0:T(8,128)(2,1)} fusion(f32[128,1792]{1,0:T(8,128)} %collective-permute-done.3, f32[128,3584]{1,0:T(8,128)S(1)} %copy-done.5, s32[]{:T(128)S(6)} %select_n.72), kind=kLoop, calls=%fused_computation.52 | loop fusion | flops 458752 | bytes 2293764 | tf_op jit(solution)/shard_map/broadcast_in_dim | solution.py:169
  (29 shorter events, 0.3 us)
Async XLA Ops:
  0.6 49.9 %copy-start = (bf16[1,1,3584,256]{3,2,1,0:T(8,128)(2,1)S(1)}, bf16[1,1,3584,256]{3,2,1,0:T(8,128)(2,1)}, u32[]{:S(2)}) copy-start(bf16[1,1,3584,256]{3,2,1,0:T(8,128)(2,1)} %param.21) | copy-start | bytes 5505028
  0.6 16.4 %collective-permute-start.1 = (bf16[128,1792]{1,0:T(8,128)(2,1)}, bf16[128,1792]{1,0:T(8,128)(2,1)}, u32[]{:S(2)}, u32[]{:S(2)}) collective-permute-start(bf16[128,1792]{1,0:T(8,128)(2,1)} %bitcast.127), channel_id=1, source_target_pairs={{8,0},{16,8},{24,16},{0,24},{9,1},{17,9},{25,17},{1,25},{10,2},{18... | collective-permute-start | bytes 1376264 | tf_op jit(solution)/shard_map/ppermute | solution.py:10
  5.8 20.7 %collective-permute-start = (bf16[128,1792]{1,0:T(8,128)(2,1)}, bf16[128,1792]{1,0:T(8,128)(2,1)S(1)}, u32[]{:S(2)}, u32[]{:S(2)}) collective-permute-start(bf16[128,1792]{1,0:T(8,128)(2,1)} %bitcast.128), channel_id=1, source_target_pairs={{24,0},{0,8},{8,16},{16,24},{25,1},{1,9},{9,17},{17,25},{26,2},{2,... | collective-permute-start | bytes 1376264 | tf_op jit(solution)/shard_map/ppermute | solution.py:10
  9.5 3.0 %copy-start.2 = (bf16[1,128,3584]{2,1,0:T(8,128)(2,1)}, bf16[1,128,3584]{2,1,0:T(8,128)(2,1)S(1)}, u32[]{:S(2)}) copy-start(bf16[1,128,3584]{2,1,0:T(8,128)(2,1)S(1)} %all-gather) | copy-start | bytes 2752516
  19.7 2.4 %copy-start.3 = (bf16[128,3584]{1,0:T(8,128)(2,1)}, bf16[128,3584]{1,0:T(8,128)(2,1)S(1)}, u32[]{:S(2)}) copy-start(bf16[128,3584]{1,0:T(8,128)(2,1)S(1)} %all_gather.11) | copy-start | bytes 2752516
  31.1 14.3 %all-to-all-start = ((bf16[3,4,4,3584]{3,2,0,1:T(4,128)(2,1)}), bf16[3,4,4,3584]{3,2,0,1:T(4,128)(2,1)}, u32[]{:S(2)}, u32[]{:S(2)}) async-start(bf16[3,4,4,3584]{3,2,0,1:T(4,128)(2,1)} %bitcast.11), calls=%async_computation | async-start | bytes 688128 | tf_op jit(solution)/shard_map/all_to_all | solution.py:143
  47.8 2.3 %copy-start.1 = (bf16[1,1,3584,256]{3,2,1,0:T(8,128)(2,1)S(1)}, bf16[1,1,3584,256]{3,2,1,0:T(8,128)(2,1)}, u32[]{:S(2)}) copy-start(bf16[1,1,3584,256]{3,2,1,0:T(8,128)(2,1)} %param.20) | copy-start | bytes 5505028
  63.4 9.8 %all-to-all-start.1 = ((bf16[2,4,4,3584]{3,2,0,1:T(4,128)(2,1)}), bf16[2,4,4,3584]{3,2,0,1:T(4,128)(2,1)}, u32[]{:S(2)}, u32[]{:S(2)}) async-start(bf16[2,4,4,3584]{3,2,0,1:T(4,128)(2,1)} %pad_maximum_fusion), calls=%async_computation.1 | async-start | bytes 458752 | tf_op jit(solution)/shard_map/all_to_all | solution.py:146
  85.3 2.2 %copy-start.7 = (bf16[1,4,4,3584]{3,2,0,1:T(4,128)(2,1)S(1)}, bf16[1,4,4,3584]{3,2,0,1:T(4,128)(2,1)}, u32[]{:S(2)}) copy-start(bf16[1,4,4,3584]{3,2,0,1:T(4,128)(2,1)} %get-tuple-element.9) | copy-start | bytes 344068
  87.5 7.7 %collective-permute-start.2 = (f32[128,1792]{1,0:T(8,128)}, f32[128,1792]{1,0:T(8,128)S(1)}, u32[]{:S(2)}, u32[]{:S(2)}) collective-permute-start(f32[128,1792]{1,0:T(8,128)} %constant_dynamic-slice_fusion), channel_id=1, source_target_pairs={{1,0},{0,1},{3,2},{2,3},{5,4},{4,5},{7,6},{6,7},{9,8},{8,9},{11,10... | collective-permute-start | bytes 2752520 | tf_op jit(solution)/shard_map/ppermute | solution.py:10
  87.6 1.5 %copy-start.6 = (f32[128,3584]{1,0:T(8,128)S(1)}, f32[128,3584]{1,0:T(8,128)}, u32[]{:S(2)}) copy-start(f32[128,3584]{1,0:T(8,128)} %fusion.11) | copy-start | bytes 5505028
  92.4 1.3 %copy-start.4 = (f32[128,3584]{1,0:T(8,128)}, f32[128,3584]{1,0:T(8,128)S(1)}, u32[]{:S(2)}) copy-start(f32[128,3584]{1,0:T(8,128)S(1)} %fusion) | copy-start | bytes 5505028
  94.7 2.9 %collective-permute-start.3 = (f32[128,1792]{1,0:T(8,128)}, f32[128,1792]{1,0:T(8,128)}, u32[]{:S(2)}, u32[]{:S(2)}) collective-permute-start(f32[128,1792]{1,0:T(8,128)} %constant_dynamic-slice_fusion.1), channel_id=1, source_target_pairs={{1,0},{0,1},{3,2},{2,3},{5,4},{4,5},{7,6},{6,7},{9,8},{8,9},{11,10... | collective-permute-start | bytes 2752520 | tf_op jit(solution)/shard_map/ppermute | solution.py:10
  95.2 2.4 %copy-start.5 = (f32[128,3584]{1,0:T(8,128)S(1)}, f32[128,3584]{1,0:T(8,128)}, u32[]{:S(2)}) copy-start(f32[128,3584]{1,0:T(8,128)} %copy-done.4) | copy-start | bytes 5505028
where the time goes:
time: 101 us; the launch traced here: 99.7 us
  matrix products  42.3 us (42%)
  local copies, waits for them, and re-layouts  15.7 us (16%)
  starting transfers between devices  13.9 us (14%)
  waiting for transfers between devices  12.2 us (12%)
  blocking collectives  7.79 us (8%)
  other arithmetic  7.08 us (7%)
    dot_general x6, matrix products, contract_last(): lax.dot_general(left, right, (((1,), (1,)), ((), ())), preferred_element_...  20.8 us
    ppermute x4, waiting for transfers between devices, passed_along(): return lax.ppermute(block, axis, route)  9.2 us
    dot_general x1, matrix products, shared_pass(): shared_out = jnp.dot(hidden, down_w, preferred_element_type=jnp.float32)  6.2 us
    ppermute x4, starting transfers between devices, passed_along(): return lax.ppermute(block, axis, route)  5.64 us
    all_to_all x1, starting transfers between devices, local(): lax.all_to_all(jnp.stack((result, grad_rows)).reshape(2, n_expert, capaci...  4.14 us
    all_to_all x1, starting transfers between devices, local(): lax.all_to_all(parcel, 'expert', split_axis=1, concat_axis=1, tiled=True)  4.1 us
    dot_general x1, matrix products, expert_local(): jnp.dot(hidden, down_w, preferred_element_type=jnp.float32)  3.3 us
    dynamic_slice x2, local copies, waits for them, and re-layouts, other_sums(): piece = lax.dynamic_slice_in_dim(total, to * width, width, axis=1)  3.22 us
  transfers between devices with their start and end apart: 6, of which 4 were waited for; matrix products, arithmetic and copies ran while one was open for 26% of the time, Pallas kernels for 0%

commit v1 on v0

--- a/solution.py
+++ b/solution.py
@@ -127,8 +127,13 @@
     up_w = up_routed[0, 0]
     down_w = down_routed[0, 0]
     full_saved = lax.all_gather(saved_input[0], "tensor", axis=1, tiled=True)
-    full_in = lax.all_gather(forward_in, "tensor", axis=1, tiled=True)
-    full_cot = lax.all_gather(backward_in, "tensor", axis=1, tiled=True)
+    full_in, full_cot = jnp.split(
+        lax.all_gather(
+            jnp.concatenate([forward_in, backward_in], axis=0), "tensor", axis=1, tiled=True
+        ),
+        [forward_in.shape[0]],
+        axis=0,
+    )
     feature_count = full_in.shape[1]
     weight_b = jnp.sum(level_b, axis=1).astype(jnp.float32) / 4096.0
     parcel = jnp.stack(

time: 101 us -> 114 us (1.13)
  waiting for transfers between devices: 12.2 us -> 27.1 us
  between operations: 0.82 us -> 14.3 us
  local copies, waits for them, and re-layouts: 15.7 us -> 7.08 us
  blocking collectives: 7.79 us -> 2.46 us
    ppermute x4, waiting for transfers between devices: 9.2 us -> 20.2 us  [passed_along(): return lax.ppermute(block, axis, route)]
    all_gather x2 -> x0, blocking collectives: 5.11 us -> none  [the longest x1 2.66 us: local(): full_cot = lax.all_gather(backward_in, 'tensor', axis=1, tiled=True)]
    all_gather x0 -> x1, waiting for transfers between devices: none -> 4.5 us  [local(): lax.all_gather(jnp.concatenate([forward_in, backward_in], axis=0), 'tenso...]
    dot_general x6, matrix products: 20.8 us -> 18.2 us  [contract_last(): lax.dot_general(left, right, (((1,), (1,)), ((), ())), preferred_element_...]
    dot_general x3, matrix products: 1.35 us -> 3.02 us  [select_rows(): return jnp.dot(chosen, values, preferred_element_type=jnp.float32)]
    slice x1, local copies, waits for them, and re-layouts: 1.72 us -> 0.08 us  [local(): routed_grad = combine(doubled(chosen_b), back[1])]
    squeeze x1, local copies, waits for them, and re-layouts: 1.57 us -> 0.03 us  [local(): routed_out = combine(factors_f, jnp.concatenate((back[0], back[0]), axis=0))]
    dot_general x1, matrix products: 0.38 us -> 1.85 us  [expert_local(): gate_back = jnp.dot(rows_saved, gate_w, preferred_element_type=jnp.float32)]
  transfers between devices with their start and end apart: 6 -> 7, of which waited for: 4 -> 5; matrix products, arithmetic and copies ran while one was open for 26% -> 20% of each run, Pallas kernels for 0% -> 0%
where the time goes in v1:
time: 114 us; the launch traced here: 113 us
  matrix products  41.7 us (37%)
  waiting for transfers between devices  27.1 us (24%)
  between operations  14.3 us (13%)
  starting transfers between devices  14 us (12%)
  local copies, waits for them, and re-layouts  7.08 us (6%)
  other arithmetic  6.46 us (6%)
  blocking collectives  2.46 us (2%)
    ppermute x4, waiting for transfers between devices, passed_along(): return lax.ppermute(block, axis, route)  20.2 us
    dot_general x6, matrix products, contract_last(): lax.dot_general(left, right, (((1,), (1,)), ((), ())), preferred_element_...  18.2 us
    dot_general x1, matrix products, shared_pass(): shared_out = jnp.dot(hidden, down_w, preferred_element_type=jnp.float32)  6.43 us
    ppermute x4, starting transfers between devices, passed_along(): return lax.ppermute(block, axis, route)  5.71 us
    all_gather x1, waiting for transfers between devices, local(): lax.all_gather(jnp.concatenate([forward_in, backward_in], axis=0), 'tenso...  4.5 us
    all_to_all x1, starting transfers between devices, local(): lax.all_to_all(jnp.stack((result, grad_rows)).reshape(2, n_expert, capaci...  4.13 us
    all_to_all x1, starting transfers between devices, local(): lax.all_to_all(parcel, 'expert', split_axis=1, concat_axis=1, tiled=True)  4.1 us
    dynamic_slice x2, local copies, waits for them, and re-layouts, other_sums(): piece = lax.dynamic_slice_in_dim(total, to * width, width, axis=1)  3.31 us
  transfers between devices with their start and end apart: 7, of which 5 were waited for; matrix products, arithmetic and copies ran while one was open for 20% of the time, Pallas kernels for 0%

profile of v1, /device:TPU:0, one launch (start us, length us, event | category | flops | bytes accessed | tf_op | source)
XLA Modules:
  0.0 113.1 jit_solution(10842644721731530854)
XLA Ops:
  7.2 0.0 copy-start
  7.2 0.0 all-gather.3.cloned.1.call-start
  7.3 3.1 %collective-permute-start = (bf16[128,1792]{1,0:T(8,128)(2,1)}, bf16[128,1792]{1,0:T(8,128)(2,1)S(1)}, u32[]{:S(2)}, u32[]{:S(2)}) collective-permute-start(bf16[128,1792]{1,0:T(8,128)(2,1)} %bitcast.124), channel_id=1, source_target_pairs={{24,0},{0,8},{8,16},{16,24},{25,1},{1,9},{9,17},{17,25},{26,2},{2,... | collective-permute-start | bytes 1376264 | tf_op jit(solution)/shard_map/ppermute | solution.py:10
  10.4 2.1 %collective-permute-start.1 = (bf16[128,1792]{1,0:T(8,128)(2,1)}, bf16[128,1792]{1,0:T(8,128)(2,1)S(1)}, u32[]{:S(2)}, u32[]{:S(2)}) collective-permute-start(bf16[128,1792]{1,0:T(8,128)(2,1)} %bitcast.125), channel_id=1, source_target_pairs={{8,0},{16,8},{24,16},{0,24},{9,1},{17,9},{25,17},{1,25},{10,2},{18... | collective-permute-start | bytes 1376264 | tf_op jit(solution)/shard_map/ppermute | solution.py:10
  12.5 11.6 %collective-permute-done = bf16[128,1792]{1,0:T(8,128)(2,1)S(1)} collective-permute-done((bf16[128,1792]{1,0:T(8,128)(2,1)}, bf16[128,1792]{1,0:T(8,128)(2,1)S(1)}, u32[]{:S(2)}, u32[]{:S(2)}) %collective-permute-start) | collective-permute-done | bytes 458784 | tf_op jit(solution)/shard_map/ppermute | solution.py:10
  24.0 8.4 %collective-permute-done.1 = bf16[128,1792]{1,0:T(8,128)(2,1)S(1)} collective-permute-done((bf16[128,1792]{1,0:T(8,128)(2,1)}, bf16[128,1792]{1,0:T(8,128)(2,1)S(1)}, u32[]{:S(2)}, u32[]{:S(2)}) %collective-permute-start.1) | collective-permute-done | bytes 458784 | tf_op jit(solution)/shard_map/ppermute | solution.py:10
  32.4 1.0 pad_maximum_fusion
  33.4 0.0 all-gather.3.cloned.1.call-update
  33.5 0.2 select_reduce_fusion
  33.7 0.0 copy-done.4
  33.7 2.5 %all-gather = bf16[1,128,3584]{2,1,0:T(8,128)(2,1)S(1)} all-gather(bf16[1,128,1792]{2,1,0:T(8,128)(2,1)S(1)} %copy-done.4), channel_id=2, replica_groups=mesh['pipe'=4,'expert'=4,'tensor'=2] {'tensor'}, dimensions={2}, use_global_device_ids=true | all-gather | bytes 1376256 | tf_op jit(solution)/shard_map/all_gather | solution.py:129
  36.2 0.2 convolution_convert_fusion.1
  36.5 2.7 %fusion.13 = f32[128,512]{1,0:T(8,128)S(1)} fusion(bf16[1,3584,512]{2,1,0:T(8,128)(2,1)} %param.23, bf16[1,128,3584]{2,1,0:T(8,128)(2,1)S(1)} %all-gather), kind=kOutput, calls=%fused_computation.20 | convolution fusion | flops 469762048 | bytes 4849664 | tf_op jit(solution)/shard_map/dot_general | solution.py:89
  39.2 4.5 %all-gather.3.cloned.1.call-done = bf16[256,3584]{1,0:T(8,128)(2,1)} async-done(((bf16[256,1792]{1,0:T(8,128)(2,1)}), bf16[256,3584]{1,0:T(8,128)(2,1)}) %all-gather.3.cloned.1.call-update) | async-done | bytes 1835024 | tf_op jit(solution)/shard_map/all_gather | solution.py:131
  43.7 1.4 %convolution_convert_fusion.2 = bf16[8,3584]{1,0:T(8,128)(2,1)S(1)} fusion(bf16[256,3584]{1,0:T(8,128)(2,1)} %all-gather.3.cloned.1.call-done, s32[8,128]{1,0:T(8,128)S(1)} %get-tuple-element.3), kind=kOutput, calls=%fused_computation.9 | convolution fusion | flops 7369728 | bytes 978944 | tf_op jit(solution)/shard_map/dot_general | solution.py:42
  45.2 1.4 %fusion.2 = bf16[8,3584]{1,0:T(8,128)(2,1)S(1)} fusion(bf16[8,128]{1,0:T(8,128)(2,1)S(1)} %convert_element_type.101, bf16[256,3584]{1,0:T(8,128)(2,1)} %all-gather.3.cloned.1.call-done, f32[8]{0:T(128)S(1)} %convert_multiply_fusion), kind=kOutput, calls=%fused_computation.7 | convolution fusion | flops 7397376 | bytes 976928 | tf_op jit(solution)/shard_map/dot_general | solution.py:42
  46.6 0.1 maximum_bitcast_fusion
  46.7 0.1 copy.26
  46.8 0.8 broadcast_in_dim.69
  47.6 4.1 %all-to-all-start = ((bf16[3,4,4,3584]{3,2,0,1:T(4,128)(2,1)}), bf16[3,4,4,3584]{3,2,0,1:T(4,128)(2,1)}, u32[]{:S(2)}, u32[]{:S(2)}) async-start(bf16[3,4,4,3584]{3,2,0,1:T(4,128)(2,1)} %bitcast.11), calls=%async_computation | async-start | bytes 688128 | tf_op jit(solution)/shard_map/all_to_all | solution.py:148
  51.7 3.6 %fusion.3 = f32[128,512]{1,0:T(8,128)S(1)} fusion(bf16[1,512,3584]{2,1,0:T(8,128)(2,1)} %param.25, bf16[256,3584]{1,0:T(8,128)(2,1)} %all-gather.3.cloned.1.call-done), kind=kOutput, calls=%fused_computation.10 | convolution fusion | flops 469762048 | bytes 4849664 | tf_op jit(solution)/shard_map/dot_general | solution.py:23
  55.3 6.3 %fusion.11 = f32[128,3584]{1,0:T(8,128)} fusion(bf16[1,3584,512]{2,1,0:T(8,128)(2,1)} %param.23, f32[128,512]{1,0:T(8,128)S(1)} %fusion.3, bf16[1,3584,512]{2,1,0:T(8,128)(2,1)} %param.24, bf16[1,128,3584]{2,1,0:T(8,128)(2,1)S(1)} %all-gather, f32[128,512]{1,0:T(8,128)S(1)} %fusion.13), kind=kOutput, calls=%fused_computation.18 | convolution fusion | flops 940179456 | bytes 10616832 | tf_op jit(solution)/shard_map/dot_general | solution.py:23
  61.6 0.0 all-to-all-done
  61.6 1.1 fusion.127
  62.8 1.8 %fusion.29 = f32[16,256]{1,0:T(8,128)S(1)} fusion(bf16[16,3584]{1,0:T(8,128)(2,1)S(1)} %squeeze.52, bf16[1,1,3584,256]{3,2,1,0:T(8,128)(2,1)} %param.20), kind=kOutput, calls=%fused_computation.36 | convolution fusion | flops 29360128 | bytes 1966080 | tf_op jit(solution)/shard_map/dot_general | solution.py:69
  64.6 2.6 %convolution_convert_fusion = bf16[16,3584]{1,0:T(8,128)(2,1)S(1)} fusion(bf16[1,1,256,3584]{3,2,1,0:T(8,128)(2,1)} %param.22, bf16[16,3584]{1,0:T(8,128)(2,1)S(1)} %squeeze.52, bf16[1,1,3584,256]{3,2,1,0:T(8,128)(2,1)S(1)} %copy-done, f32[16,256]{1,0:T(8,128)S(1)} %fusion.29), kind=kOutput, calls=%fused_computation.5 | convolution fusion | flops 58802176 | bytes 3915776 | tf_op jit(solution)/shard_map/dot_general | solution.py:72
  67.4 1.8 %fusion.27 = f32[16,256]{1,0:T(8,128)S(1)} fusion(bf16[16,3584]{1,0:T(8,128)(2,1)S(1)} %squeeze.57, bf16[1,1,3584,256]{3,2,1,0:T(8,128)(2,1)} %param.20), kind=kOutput, calls=%fused_computation.34 | convolution fusion | flops 29360128 | bytes 1966080 | tf_op jit(solution)/shard_map/dot_general | solution.py:73
  69.3 2.1 %fusion.17 = f32[16,256]{1,0:T(8,128)S(1)} fusion(bf16[16,3584]{1,0:T(8,128)(2,1)S(1)} %squeeze.56, bf16[1,1,256,3584]{3,2,1,0:T(8,128)(2,1)} %param.22), kind=kOutput, calls=%fused_computation.24 | convolution fusion | flops 29360128 | bytes 1966080 | tf_op jit(solution)/shard_map/dot_general | solution.py:23
  71.3 2.8 %fusion.25 = f32[16,3584]{1,0:T(8,128)S(1)} fusion(bf16[1,1,3584,256]{3,2,1,0:T(8,128)(2,1)} %param.20, f32[16,256]{1,0:T(8,128)S(1)} %fusion.17, bf16[16,3584]{1,0:T(8,128)(2,1)S(1)} %squeeze.57, bf16[1,1,3584,256]{3,2,1,0:T(8,128)(2,1)S(1)} %copy-done, f32[16,256]{1,0:T(8,128)S(1)} %fusion.27), kind=kOutput, calls=%fused_computation.32 | convolution fusion | flops 58761216 | bytes 4046848 | tf_op jit(solution)/shard_map/dot_general | solution.py:23
  74.1 0.6 fusion.1
  74.8 0.8 pad_maximum_fusion.1
  75.6 4.1 %all-to-all-start.1 = ((bf16[2,4,4,3584]{3,2,0,1:T(4,128)(2,1)}), bf16[2,4,4,3584]{3,2,0,1:T(4,128)(2,1)S(1)}, u32[]{:S(2)}, u32[]{:S(2)}) async-start(bf16[2,4,4,3584]{3,2,0,1:T(4,128)(2,1)} %pad_maximum_fusion.1), calls=%async_computation.1 | async-start | bytes 458752 | tf_op jit(solution)/shard_map/all_to_all | solution.py:151
  79.7 3.0 %fusion.15 = f32[128,512]{1,0:T(8,128)S(1)} fusion(bf16[1,3584,512]{2,1,0:T(8,128)(2,1)} %param.23, bf16[256,3584]{1,0:T(8,128)(2,1)} %all-gather.3.cloned.1.call-done), kind=kOutput, calls=%fused_computation.22 | convolution fusion | flops 469762048 | bytes 4849664 | tf_op jit(solution)/shard_map/dot_general | solution.py:85
  82.7 2.4 %all-to-all-done.1 = bf16[2,4,4,3584]{3,2,0,1:T(4,128)(2,1)S(1)} async-done(((bf16[2,4,4,3584]{3,2,0,1:T(4,128)(2,1)}), bf16[2,4,4,3584]{3,2,0,1:T(4,128)(2,1)S(1)}, u32[]{:S(2)}, u32[]{:S(2)}) %all-to-all-start.1) | async-done | bytes 229408 | tf_op jit(solution)/shard_map/all_to_all | solution.py:151
  85.1 0.1 fusion.128
  85.3 1.7 %fusion.90 = f32[128,3584]{1,0:T(8,128)} fusion(bf16[16,3584]{1,0:T(8,128)(2,1)S(1)} %squeeze.58, bf16[16,128]{1,0:T(8,128)(2,1)S(1)} %bitcast.121, bf16[16,128]{1,0:T(8,128)(2,1)S(1)} %bitcast.120), kind=kOutput, calls=%fused_computation.73 | convolution fusion | flops 29835264 | bytes 1957888 | tf_op jit(solution)/shard_map/dot_general | solution.py:52
  86.9 6.4 %convolution_add_fusion.1 = f32[128,3584]{1,0:T(8,128)} fusion(f32[128,3584]{1,0:T(8,128)} %fusion.90, bf16[1,512,3584]{2,1,0:T(8,128)(2,1)} %param.25, bf16[1,3584,512]{2,1,0:T(8,128)(2,1)} %param.24, bf16[256,3584]{1,0:T(8,128)(2,1)} %all-gather.3.cloned.1.call-done, f32[128,512]{1,0:T(8,128)S(1)} %fusion.15), kind=kOutput, calls=%fused_computation.2 | convolution fusion | flops 940376064 | bytes 12189696 | tf_op jit(solution)/shard_map/dot_general | solution.py:88
  93.4 2.3 %constant_dynamic-slice_fusion = f32[128,1792]{1,0:T(8,128)} fusion(f32[128,3584]{1,0:T(8,128)} %convolution_add_fusion.1, s32[]{:T(128)S(6)} %select_n.74), kind=kLoop, calls=%fused_computation.125 | loop fusion | bytes 1835012 | tf_op jit(solution)/shard_map/dynamic_slice | solution.py:63
  95.7 0.0 collective-permute-start.2
  95.7 0.4 fusion.129
  96.1 2.8 %fusion = f32[128,3584]{1,0:T(8,128)S(1)} fusion(f32[128,3584]{1,0:T(8,128)S(1)} %fusion.129, f32[128,3584]{1,0:T(8,128)} %fusion.11, bf16[1,3584,512]{2,1,0:T(8,128)(2,1)S(1)} %copy-done.1, f32[128,512]{1,0:T(8,128)S(1)} %fusion.3, f32[128,512]{1,0:T(8,128)S(1)} %fusion.13), kind=kOutput, calls=%fused_computation.1 | convolution fusion | flops 471072768 | bytes 9699328 | tf_op jit(solution)/shard_map/dot_general | solution.py:23
  99.0 1.3 %copy-done.2 = f32[128,3584]{1,0:T(8,128)} copy-done((f32[128,3584]{1,0:T(8,128)}, f32[128,3584]{1,0:T(8,128)S(1)}, u32[]{:S(2)}) %copy-start.2) | copy-done | bytes 1835032
  100.2 1.0 constant_dynamic-slice_fusion.1
  101.2 0.5 collective-permute-start.3
  101.7 0.0 collective-permute-done.2
  101.8 2.2 %fusion.79 = bf16[1,128,1792]{2,1,0:T(8,128)(2,1)} fusion(f32[128,1792]{1,0:T(8,128)S(1)} %collective-permute-done.2, f32[128,3584]{1,0:T(8,128)} %convolution_add_fusion.1, s32[]{:T(128)S(6)} %select_n.72), kind=kLoop, calls=%fused_computation.59 | loop fusion | flops 458752 | bytes 2293764 | tf_op jit(solution)/shard_map/broadcast_in_dim | solution.py:174
  103.9 0.3 collective-permute-done.3
  104.2 2.0 %fusion.80 = bf16[1,128,1792]{2,1,0:T(8,128)(2,1)} fusion(f32[128,1792]{1,0:T(8,128)} %collective-permute-done.3, f32[128,3584]{1,0:T(8,128)S(1)} %copy-done.3, s32[]{:T(128)S(6)} %select_n.72), kind=kLoop, calls=%fused_computation.60 | loop fusion | flops 458752 | bytes 2293764 | tf_op jit(solution)/shard_map/broadcast_in_dim | solution.py:174
  (33 shorter events, 0.5 us)
Async XLA Ops:
  7.2 57.5 %copy-start = (bf16[1,1,3584,256]{3,2,1,0:T(8,128)(2,1)S(1)}, bf16[1,1,3584,256]{3,2,1,0:T(8,128)(2,1)}, u32[]{:S(2)}) copy-start(bf16[1,1,3584,256]{3,2,1,0:T(8,128)(2,1)} %param.21) | copy-start | bytes 5505028
  7.2 26.3 %copy-start.5 = (s32[2,1,128,8]{2,3,1,0:T(8,128)S(1)}, s32[2,1,128,8]{2,3,1,0:T(8,128)}, u32[]{:S(2)}) copy-start(s32[2,1,128,8]{2,3,1,0:T(8,128)} %param.19) | copy-start | bytes 24580
  7.2 26.3 %copy-start.6 = (s32[2,1,128,8]{2,3,1,0:T(8,128)S(1)}, s32[2,1,128,8]{2,3,1,0:T(8,128)}, u32[]{:S(2)}) copy-start(s32[2,1,128,8]{2,3,1,0:T(8,128)} %param.18) | copy-start | bytes 24580
  7.2 26.3 %copy-start.8 = (s32[2,1,128,8]{2,3,1,0:T(8,128)S(1)}, s32[2,1,128,8]{2,3,1,0:T(8,128)}, u32[]{:S(2)}) copy-start(s32[2,1,128,8]{2,3,1,0:T(8,128)} %param.17) | copy-start | bytes 24580
  7.2 26.3 %copy-start.7 = (s32[2,1,128,8]{2,3,1,0:T(8,128)S(1)}, s32[2,1,128,8]{2,3,1,0:T(8,128)}, u32[]{:S(2)}) copy-start(s32[2,1,128,8]{2,3,1,0:T(8,128)} %param.16) | copy-start | bytes 24580
  7.2 26.5 %copy-start.4 = (bf16[1,128,1792]{2,1,0:T(8,128)(2,1)S(1)}, bf16[1,128,1792]{2,1,0:T(8,128)(2,1)}, u32[]{:S(2)}) copy-start(bf16[1,128,1792]{2,1,0:T(8,128)(2,1)} %param.15) | copy-start | bytes 1376260
  7.2 36.5 %all-gather.3.cloned.1.call-start = ((), (), s32[]{:S(2)}) async-start(), calls=%async_computation.2 | async-start | bytes 2752512 | tf_op jit(solution)/shard_map/all_gather | solution.py:131
  7.3 16.8 %collective-permute-start = (bf16[128,1792]{1,0:T(8,128)(2,1)}, bf16[128,1792]{1,0:T(8,128)(2,1)S(1)}, u32[]{:S(2)}, u32[]{:S(2)}) collective-permute-start(bf16[128,1792]{1,0:T(8,128)(2,1)} %bitcast.124), channel_id=1, source_target_pairs={{24,0},{0,8},{8,16},{16,24},{25,1},{1,9},{9,17},{17,25},{26,2},{2,... | collective-permute-start | bytes 1376264 | tf_op jit(solution)/shard_map/ppermute | solution.py:10
  10.4 22.0 %collective-permute-start.1 = (bf16[128,1792]{1,0:T(8,128)(2,1)}, bf16[128,1792]{1,0:T(8,128)(2,1)S(1)}, u32[]{:S(2)}, u32[]{:S(2)}) collective-permute-start(bf16[128,1792]{1,0:T(8,128)(2,1)} %bitcast.125), channel_id=1, source_target_pairs={{8,0},{16,8},{24,16},{0,24},{9,1},{17,9},{25,17},{1,25},{10,2},{18... | collective-permute-start | bytes 1376264 | tf_op jit(solution)/shard_map/ppermute | solution.py:10
  47.6 14.0 %all-to-all-start = ((bf16[3,4,4,3584]{3,2,0,1:T(4,128)(2,1)}), bf16[3,4,4,3584]{3,2,0,1:T(4,128)(2,1)}, u32[]{:S(2)}, u32[]{:S(2)}) async-start(bf16[3,4,4,3584]{3,2,0,1:T(4,128)(2,1)} %bitcast.11), calls=%async_computation | async-start | bytes 688128 | tf_op jit(solution)/shard_map/all_to_all | solution.py:148
  75.6 9.5 %all-to-all-start.1 = ((bf16[2,4,4,3584]{3,2,0,1:T(4,128)(2,1)}), bf16[2,4,4,3584]{3,2,0,1:T(4,128)(2,1)S(1)}, u32[]{:S(2)}, u32[]{:S(2)}) async-start(bf16[2,4,4,3584]{3,2,0,1:T(4,128)(2,1)} %pad_maximum_fusion.1), calls=%async_computation.1 | async-start | bytes 458752 | tf_op jit(solution)/shard_map/all_to_all | solution.py:151
  93.4 2.8 %copy-start.1 = (bf16[1,3584,512]{2,1,0:T(8,128)(2,1)S(1)}, bf16[1,3584,512]{2,1,0:T(8,128)(2,1)}, u32[]{:S(2)}) copy-start(bf16[1,3584,512]{2,1,0:T(8,128)(2,1)} %param.24) | copy-start | bytes 11010052
  95.7 6.1 %collective-permute-start.2 = (f32[128,1792]{1,0:T(8,128)}, f32[128,1792]{1,0:T(8,128)S(1)}, u32[]{:S(2)}, u32[]{:S(2)}) collective-permute-start(f32[128,1792]{1,0:T(8,128)} %constant_dynamic-slice_fusion), channel_id=1, source_target_pairs={{1,0},{0,1},{3,2},{2,3},{5,4},{4,5},{7,6},{6,7},{9,8},{8,9},{11,10... | collective-permute-start | bytes 2752520 | tf_op jit(solution)/shard_map/ppermute | solution.py:10
  99.0 1.3 %copy-start.2 = (f32[128,3584]{1,0:T(8,128)}, f32[128,3584]{1,0:T(8,128)S(1)}, u32[]{:S(2)}) copy-start(f32[128,3584]{1,0:T(8,128)S(1)} %fusion) | copy-start | bytes 5505028
  101.2 3.0 %collective-permute-start.3 = (f32[128,1792]{1,0:T(8,128)}, f32[128,1792]{1,0:T(8,128)}, u32[]{:S(2)}, u32[]{:S(2)}) collective-permute-start(f32[128,1792]{1,0:T(8,128)} %constant_dynamic-slice_fusion.1), channel_id=1, source_target_pairs={{1,0},{0,1},{3,2},{2,3},{5,4},{4,5},{7,6},{6,7},{9,8},{8,9},{11,10... | collective-permute-start | bytes 2752520 | tf_op jit(solution)/shard_map/ppermute | solution.py:10
  101.7 2.4 %copy-start.3 = (f32[128,3584]{1,0:T(8,128)S(1)}, f32[128,3584]{1,0:T(8,128)}, u32[]{:S(2)}) copy-start(f32[128,3584]{1,0:T(8,128)} %copy-done.2) | copy-start | bytes 5505028
Sparse Core Ops, SparseCore 0:
  33.5 10.1 all-gather.2
